TPU v7x, 8 devices: a whole 2x2x1 slice. The times are simulated.
8 devices in a mesh: dp: 1 (over z), ch: 2 (over y), wd: 4 (over x, core).
Axes of the slice: x: 2, y: 2, z: 1, core: 2. Of those that a mesh axis runs over, the one named last changes fastest.
Arguments:
- resid_in: bfloat16 [16384, 2048], P('dp', 'wd')
- seg_pos: int32 [4, 4096], P('dp')
- gain_temporal: bfloat16 [2048], P('wd')
- w_x: bfloat16 [2048, 2560], P('wd', 'ch')
- bias_x: bfloat16 [2560], P('ch')
- w_y: bfloat16 [2048, 2560], P('wd', 'ch')
- bias_y: bfloat16 [2560], P('ch')
- conv_w: bfloat16 [4, 2560], P(None, 'ch')
- conv_bias: bfloat16 [2560], P('ch')
- lam_param: float32 [2560], P('ch')
- rgate_w: bfloat16 [10, 256, 256], P('ch')
- rgate_b: bfloat16 [2560], P('ch')
- igate_w: bfloat16 [10, 256, 256], P('ch')
- igate_b: bfloat16 [2560], P('ch')
- w_o: bfloat16 [2560, 2048], P('ch', 'wd')
- bias_o: bfloat16 [2048], P('wd')
- gain_mlp: bfloat16 [2048], P('wd')
- w_g: bfloat16 [2048, 6144], P('wd', 'ch')
- bias_g: bfloat16 [6144], P('ch')
- w_u: bfloat16 [2048, 6144], P('wd', 'ch')
- bias_u: bfloat16 [6144], P('ch')
- w_d: bfloat16 [6144, 2048], P('ch', 'wd')
- bias_d: bfloat16 [2048], P('wd')
Outputs:
- output: bfloat16 [16384, 2048], P('dp', 'wd')
All inputs are finite; a program needn't handle non-finite values.
Results may differ from a plain program's by a relative error of at most 0.0129377.
Values are sent between devices in bfloat16 or wider.
A program may use at most 1 GiB of HBM per device.

v0:
```python
import jax
import jax.numpy as jnp
from jax import lax
from jax.experimental import pallas as pl
from jax.experimental.pallas import tpu as pltpu
from jax.sharding import PartitionSpec as P

MESH = pl.DeviceIdType.MESH
F32, BF16 = jnp.float32, jnp.bfloat16
EPS = 1e-6
LANES = 256
CHUNK = 256
SUB = 8
EDGE = 24
ROW = 128
UP = 512
DOWN = 2
NEAR = 224
NX = 4
NWD, NCH = 4, 2
NDEV = NWD * NCH
ANY = pl.BlockSpec(memory_space=pl.ANY)
VMEM_LIMIT = 65_800_000
OWN_X, OWN_Y, OWN_P, X_P, X_Y, Y_P, Y_X, D_P = range(8)


def gelu(v):
    return 0.5 * v * (1.0 + jnp.tanh(0.7978845608028654 * (v + 0.044715 * (v * v * v))))


def sigmoid(v):
    return 1.0 / (1.0 + jnp.exp(-v))


def eight(k):
    return slice(k * SUB, (k + 1) * SUB)


def shuffle_matrix(transposed):
    rows = lax.broadcasted_iota(jnp.int32, (CHUNK, CHUNK), 0)
    cols = lax.broadcasted_iota(jnp.int32, (CHUNK, CHUNK), 1)
    out, src = (cols, rows) if transposed else (rows, cols)
    return jnp.where((out % SUB) * (CHUNK // SUB) + out // SUB == src, 1.0, 0.0).astype(BF16)


def layer(resid, seg_ref, w_y, w_x, w_o, w_g, w_u, w_d, rgate, igate, small,
          out, g_y, g_x, g_o, g_g, g_u, g_d, x_far,
          n_s, acc_s, act_s, t_w, par_s, vwd_s, pos_s, u_s, h_s, prod_s, tail_s, h0_s,
          msg_out, msg_in, ssem, rsem, dssem, drsem, tsem, osem, xssem, xrsem, pssem, prsem, lsem, mssem, mrsem, xlsem, ossem, orsem, fssem, frsem, olsem):
    ch, wd = lax.axis_index("ch"), lax.axis_index("wd")
    core = lax.rem(wd, 2)
    me = ch * NWD + wd
    wx, wp = lax.rem(wd + 2, NWD), wd + 1 - 2 * core
    dev_x, dev_y, dev_p = (0, ch, wx), (0, 1 - ch, wd), (0, ch, wp)
    own, far_x, far_y, far_d = (ch, wd), (ch, wx), (1 - ch, wd), (1 - ch, wx)
    tokens, model = n_s.shape
    width = resid.shape[1]
    blocks = w_y.shape[1] // LANES
    halves = blocks * NCH
    groups = w_g.shape[1] // LANES
    steps = tokens // CHUNK
    ups = tokens // UP
    deep = w_d.shape[0] // DOWN

    def part_of(i, size):
        return pl.ds(i * size if isinstance(i, int) else pl.multiple_of(i * size, size), size)

    def cols_of(i):
        return part_of(i, LANES)

    def wide_of(k):
        return part_of(k, width)

    x_s = act_s.at[1, pl.ds(2 * LANES, CHUNK), pl.ds(0, model)]

    def gate_area(which, side):
        return act_s.at[1, pl.ds(3 * LANES, blocks * LANES), cols_of(2 * which + side)]

    def back_tile(slot):
        return act_s.at[1, cols_of(slot), pl.ds(0, model)]

    def kept(which, slot, q):
        return act_s.at[0, part_of(q, CHUNK), cols_of(2 * which + slot)]

    def remote(src, dst, device, send, recv):
        return pltpu.make_async_remote_copy(src_ref=src, dst_ref=dst, send_sem=send, recv_sem=recv, device_id=device,
                                            device_id_type=MESH)

    def first(i):
        return [(w_y, g_y, i, False), (w_x, g_x, i, False), (w_o, g_o, i, True)]

    def second(i):
        return [(w_g, g_g, i, False), (w_u, g_u, i, False)]

    def cut(unit, owner, part):
        mine, far, i, by_rows = unit
        if by_rows:
            return mine.at[cols_of(i)] if owner is None else far.at[owner[0], cols_of(i), wide_of(owner[1])]
        base, size = (0, width) if part is None else ((0, NEAR), (NEAR, width - NEAR))[part]
        if owner is None:
            return mine.at[pl.ds(base, size), cols_of(i)]
        return far.at[owner[0], pl.ds(pl.multiple_of(owner[1] * width + base, 32), size), cols_of(i)]

    def transfer(kind, g, u, unit):
        split = not unit[-1] and unit[0] is not w_y and unit[0] is not w_x
        owner, part, device = {OWN_X: (None, None, dev_x), OWN_Y: (None, None, dev_y), OWN_P: (None, None, dev_p),
                               X_P: (far_x, None, dev_p), X_Y: (far_x, 0 if split else None, dev_y),
                               Y_P: (far_y, None, dev_p), Y_X: (far_y, 1, dev_x), D_P: (far_d, None, dev_p)}[kind]
        return remote(cut(unit, owner, part), cut(unit, owner or own, part), device, ssem.at[kind, g, u], rsem.at[kind, g, u])

    def send(g, units, kinds):
        for kind in kinds:
            for u, unit in enumerate(units):
                transfer(kind, g, u, unit).start()

    def forward(g, units):
        for u, unit in enumerate(units):
            transfer(OWN_X, g, u, unit).wait_recv()
            transfer(X_Y, g, u, unit).start()
            transfer(X_P, g, u, unit).start()
        for u, unit in enumerate(units):
            transfer(OWN_Y, g, u, unit).wait_recv()
            if len(units) == NCH:
                transfer(Y_X, g, u, unit).start()
            transfer(Y_P, g, u, unit).start()

    def relay(g, units):
        for u, unit in enumerate(units):
            transfer(X_Y, g, u, unit).wait_recv()
            if len(units) == NCH:
                transfer(Y_X, g, u, unit).wait_recv()
            transfer(D_P, g, u, unit).start()

    def ready(g, units):
        for u, unit in enumerate(units):
            for kind in (OWN_P, X_P, Y_P, D_P):
                transfer(kind, g, u, unit).wait_recv()

    def drain(g, units):
        for u, unit in enumerate(units):
            for kind in range(8):
                if len(units) == NCH or kind != Y_X:
                    transfer(kind, g, u, unit).wait_send()

    both = (OWN_X, OWN_Y, OWN_P)

    def down_piece(kind, d):
        owner, device = {OWN_X: (None, dev_x), OWN_Y: (None, dev_y), OWN_P: (None, dev_p), X_P: (far_x, dev_p),
                         Y_P: (far_y, dev_p), Y_X: (far_y, dev_x), D_P: (far_d, dev_p)}[kind]
        rows = part_of(d, deep)
        at = owner or own
        far = g_d.at[at[0], rows, wide_of(at[1])]
        return remote(w_d.at[rows] if owner is None else far, far, device, dssem.at[kind, d], drsem.at[kind, d])

    def forward_down(d):
        down_piece(OWN_Y, d).wait_recv()
        down_piece(Y_X, d).start()
        down_piece(Y_P, d).start()
        down_piece(OWN_X, d).wait_recv()
        down_piece(X_P, d).start()

    def in_tiles(j, slot):
        jj, side = j // NCH, lax.rem(j, NCH)
        return [pltpu.make_async_copy(g.at[side, :, cols_of(jj)], t_w.at[2 * u + slot, pl.ds(0, model)], tsem.at[u, slot, 0])
                for u, g in enumerate((g_y, g_x))]

    def back_tiles(j, slot):
        jj, side = j // NCH, lax.rem(j, NCH)
        return [pltpu.make_async_copy(g_o.at[side, cols_of(jj)], back_tile(slot), tsem.at[2, slot, 0])]

    def up_tiles(b, slot):
        return [pltpu.make_async_copy(g.at[c, :, cols_of(b)], t_w.at[2 * u + slot, pl.ds(c * model, model)], tsem.at[u, slot, c])
                for u, g in enumerate((g_g, g_u)) for c in range(NCH)]

    def start(copies):
        for d in copies:
            d.start()

    def wait(copies):
        for d in copies:
            d.wait()

    send(0, first(0), both)
    shared = par_s.shape[1]
    tail_rows = pl.ds(small.shape[0] - vwd_s.shape[1], vwd_s.shape[1])
    small_sends = [remote(small.at[pl.ds(0, shared)], par_s.at[ch], dev_y, pssem.at[0], prsem.at[0])]
    for p in (1, 2, 3):
        small_sends.append(remote(small.at[tail_rows], vwd_s.at[wd], (0, ch, lax.rem(wd + p, NWD)), pssem.at[p], prsem.at[p]))
    small_own = [pltpu.make_async_copy(s, d, lsem.at[i]) for i, (s, d) in enumerate(
        [(small.at[pl.ds(0, shared)], par_s.at[ch]), (small.at[tail_rows], vwd_s.at[wd]), (rgate, gate_area(0, ch)), (igate, gate_area(1, ch))])]
    start(small_sends)
    start(small_own)

    tall = w_y.shape[1]
    stay = [(w_y, act_s.at[0, pl.ds(0, width), pl.ds(0, tall)], g_y.at[ch, wide_of(wd)]),
            (w_x, act_s.at[0, pl.ds(0, width), pl.ds(tall, tall)], g_x.at[ch, wide_of(wd)]),
            (w_o, n_s.at[pl.ds(0, tall), pl.ds(0, width)], g_o.at[ch, :, wide_of(wd)]),
            (w_g, act_s.at[0, pl.ds(width, width)], g_g.at[ch, wide_of(wd)]),
            (w_u, act_s.at[0, pl.ds(2 * width, width)], g_u.at[ch, wide_of(wd)])]
    stay_in = [pltpu.make_async_copy(s, v, lsem.at[5 + i]) for i, (s, v, _) in enumerate(stay)]
    stay_out = [pltpu.make_async_copy(v, d, lsem.at[10 + i]) for i, (_, v, d) in enumerate(stay)]
    start(stay_in)

    rows_x = tokens // NX

    def x_copy(p, q):
        peer = lax.rem(wd + p, NWD)
        return remote(resid.at[pl.ds((ch * NWD + peer) * tokens + q * rows_x, rows_x)], x_far.at[pl.ds(q * rows_x, rows_x), wide_of(wd)],
                      (0, ch, peer), xssem.at[p - 1, q], xrsem.at[p - 1, q])

    for q in range(NX):
        for p in (2, 1, 3):
            x_copy(p, q).start()
    for g in range(1, blocks):
        send(g, first(g), (OWN_X,))
    forward(0, first(0))
    for c, d in zip(stay_in, stay_out):
        c.wait()
        d.start()

    def gate_over(which):
        return remote((rgate, igate)[which], gate_area(which, ch), dev_y, pssem.at[4], prsem.at[4])

    def gate_on(which):
        return remote(gate_area(which, 1 - ch), gate_area(which, 1 - ch), dev_p, pssem.at[5], prsem.at[5])

    def by_core(do):
        for which in range(2):
            @pl.when(core == which)
            def _(which=which):
                do(which)

    for g in range(1, blocks):
        send(g, first(g), (OWN_Y, OWN_P))
        if g == 1:
            by_core(lambda which: gate_over(which).start())
    send(blocks, second(0), both)
    send(blocks + 1, second(1), (OWN_X,))
    send(blocks + 2, second(2), (OWN_X,))
    wait(small_own + small_sends + stay_out)
    relay(0, first(0))
    ready(0, first(0))
    start(in_tiles(0, 0))
    start(in_tiles(1, 1))

    def wide(i):
        per = width // ROW
        first_row = vwd_s.shape[1] - 4 * per + i * per
        return jnp.concatenate([vwd_s[k, first_row + r:first_row + r + 1, :] for k in range(NWD) for r in range(per)], axis=1)

    def narrow(side, base, i):
        return jnp.concatenate([par_s[side, pl.ds(base + 2 * i + r, 1), :] for r in range(2)], axis=1)

    def channel_row(j, k):
        return narrow(lax.rem(j, NCH), 2 * blocks * k, j // NCH)

    def inner_row(side, k, b):
        return narrow(side, 2 * blocks * 10 + 2 * groups * k, b)

    def x_load(c):
        for k in range(NWD):
            @pl.when(wd == k)
            def _(k=k):
                pltpu.make_async_copy(resid.at[pl.ds(me * tokens + c * CHUNK, CHUNK)], x_s.at[:, wide_of(k)], xlsem.at[k]).start()

            @pl.when(wd != k)
            def _(k=k):
                pltpu.make_async_copy(x_far.at[part_of(c, CHUNK), wide_of(k)], x_s.at[:, wide_of(k)], xlsem.at[k]).start()

        for k in range(NWD):
            pltpu.make_async_copy(x_far.at[part_of(c, CHUNK), wide_of(k)], x_s.at[:, wide_of(k)], xlsem.at[k]).wait()

    def message(i):
        return remote(msg_out.at[i], msg_in.at[i], dev_p, mssem.at[i], mrsem.at[i])

    def project(j, q, slot):
        vals = n_s[part_of(q, CHUNK), :]
        y = jnp.dot(vals, t_w[slot, 0:model], preferred_element_type=F32) + channel_row(j, 1)
        u = jnp.dot(vals, t_w[2 + slot, 0:model], preferred_element_type=F32) + channel_row(j, 0)
        return gelu(y).astype(BF16), u.astype(BF16)

    def gate_sums(j, q, u):
        def row(i):
            return channel_row(j, i)

        pos = pos_s[part_of(q, CHUNK), :]
        pos = jnp.concatenate([pos] * (LANES // pos.shape[1]), axis=1)
        u = u.astype(F32)
        u_s[EDGE:, :] = u
        sub = lax.broadcasted_iota(jnp.int32, (SUB, LANES), 0)
        last = u[CHUNK - EDGE:, :]
        for k in range(3):
            edge = jnp.where(sub == SUB - 1, tail_s[eight(k), :], last[eight(k), :])
            u_s[eight(k), :] = pltpu.roll(edge, 1, 0)
        tail_s[:] = last
        c = row(2) + u * row(3)
        for k in range(1, 4):
            c = c + jnp.where(pos >= k, u_s[pl.ds(EDGE - SUB * k, CHUNK), :], 0.0) * row(3 + k)
        c16 = c.astype(BF16)
        gates = [gate_area(which, lax.rem(j, NCH))[cols_of(j // NCH), :] for which in range(2)]
        return c16, [jnp.dot(c16, gate, preferred_element_type=F32) for gate in gates]

    def recur(j, q, y, c16, sums):
        def row(i):
            return channel_row(j, i)

        time = CHUNK // SUB
        sub = lax.broadcasted_iota(jnp.int32, (SUB, LANES), 0)
        pos = pos_s[part_of(q, CHUNK), :]
        pos = jnp.concatenate([pos] * (LANES // pos.shape[1]), axis=1)
        rate = sigmoid(sums[0] + row(8))
        inflow = 0.5 + 0.5 * jnp.tanh(0.5 * (sums[1] + row(9)))
        log_a = rate * row(7)
        a = jnp.exp(log_a)
        scale = jnp.tanh(-log_a) * (1.0 + a * a)
        scale = scale * lax.rsqrt(jnp.maximum(scale, 1e-37))
        reset = pos == 0
        a = jnp.where(reset, 0.0, a)
        b = jnp.where(reset, 1.0, scale) * inflow * c16.astype(F32)
        h, prod = b[eight(0), :], a[eight(0), :]
        for t in range(time):
            if t:
                h = a[eight(t), :] * h + b[eight(t), :]
                prod = a[eight(t), :] * prod
            h_s[eight(t), :] = h
            prod_s[eight(t), :] = prod
        for k in (1, 2, 4):
            far = sub >= k
            h = jnp.where(far, h + prod * pltpu.roll(h, k, 0), h)
            prod = jnp.where(far, prod * pltpu.roll(prod, k, 0), prod)
        before = h0_s[:]
        ends = h + prod * before
        carry = jnp.where(sub == 0, before, pltpu.roll(ends, 1, 0))
        h0_s[:] = jnp.broadcast_to(ends[SUB - 1:, :], (SUB, LANES))
        hid = h_s[:].reshape(time, SUB, LANES) + prod_s[:].reshape(time, SUB, LANES) * carry[None]
        return (hid.reshape(CHUNK, LANES) * y.astype(F32)).astype(BF16)

    def project_back(mixed, q, slot):
        acc_s[part_of(q, CHUNK), :] += jnp.dot(mixed, back_tile(slot)[:], preferred_element_type=F32)

    wait(in_tiles(0, 0))
    mix = shuffle_matrix(False)

    @pl.loop(0, steps)
    def _(c):
        @pl.when(lax.rem(c, steps // NX) == 0)
        def _():
            for p in (1, 2, 3):
                x_copy(p, c // (steps // NX)).wait_recv()

        x_load(c)
        rows = part_of(c, CHUNK)
        vals = jnp.dot(mix, x_s[:], preferred_element_type=F32)
        scale = lax.rsqrt(jnp.mean(vals * vals, axis=1, keepdims=True) + EPS)
        n_s[rows, :] = (vals * scale * (1.0 + wide(0))).astype(BF16)
        acc_s[rows, :] = vals + wide(1)
        seq = pl.ds(me // (seg_ref.shape[1] // tokens), 1)
        here = seg_ref[seq, pl.ds(pl.multiple_of(lax.rem(me, seg_ref.shape[1] // tokens) * tokens + c * CHUNK, CHUNK), CHUNK)]
        here = jnp.broadcast_to(here, (ROW, CHUNK))
        high, low = [jnp.einsum('rc,kc->rk', mix, v.astype(F32).astype(BF16), preferred_element_type=F32) for v in (here // 64, here % 64)]
        pos_s[rows, :] = (high * 64.0 + low).astype(jnp.int32)

        @pl.when(c == steps // 2)
        def _():
            by_core(lambda which: gate_over(which).wait_recv())
            by_core(lambda which: gate_on(which).start())

        kept(0, 0, c)[:], kept(1, 0, c)[:] = project(0, c, 0)

    by_core(lambda which: gate_on(which).wait())
    back_tile(1)[:] = jnp.zeros((LANES, model), BF16)

    @pl.loop(0, steps)
    def _(q):
        kept(2, 1, q)[:] = jnp.zeros((CHUNK, LANES), BF16)

    def came(i):
        return jnp.minimum(jnp.maximum(i - 5 - i // 8, 0), 4)

    def pass_on(low, high):
        @pl.loop(low, high)
        def _(b):
            forward(blocks + b, second(b))

            @pl.when(b < 6)
            def _():
                send(blocks + b + 3, second(b + 3), both)

            @pl.when((b > 6) & (b + 2 < groups))
            def _():
                send(blocks + b + 2, second(b + 2), both)

    @pl.loop(0, halves)
    def _(i):
        slot, other = lax.rem(i, 2), lax.rem(i + 1, 2)

        pass_on(came(i + core), came(i + core + 1))

        def onward_first(of):
            for at, g in ((1, 2), (2, 3), (3, 4)):
                @pl.when((core == of) & (i == at))
                def _(at=at, g=g):
                    forward(g, first(g))
                    if at > 1:
                        send(blocks + at - 1, second(at - 1), (OWN_Y, OWN_P))

        onward_first(1)
        for g, at in ((1, 0), (2, 2), (3, 4), (4, 6)):
            @pl.when((core == 1) & (i == at))
            def _(g=g):
                if g == 1:
                    forward(g, first(g))
                relay(g, first(g))

        @pl.when((core == 1) & (i == 8))
        def _():
            relay(blocks, second(0))

        @pl.when(i < halves - 1)
        def _():
            wait(in_tiles(i + 1, other))

        @pl.when((lax.rem(i, 2) == 1) & (i < halves - 2))
        def _():
            start(in_tiles(i + 2, slot))

        start(back_tiles(i, slot))

        def middle():
            onward_first(0)

            @pl.when((core == 0) & (i == 8))
            def _():
                relay(blocks, second(0))

        @pl.when(core == 0)
        def _():
            h0_s[:] = jnp.zeros_like(h0_s)
            tail_s[:] = jnp.zeros_like(tail_s)

        @pl.when(core == 1)
        def _():
            message(i).wait_recv()
            tail_s[:] = msg_in[i, :EDGE, :]
            h0_s[:] = msg_in[i, EDGE:, :]

        @pl.loop(0, steps)
        def _(q):
            @pl.when(q == steps // 2)
            def _():
                middle()

            mixed, y, u = kept(2, other, q)[:], kept(0, slot, q)[:], kept(1, slot, q)[:]
            project_back(mixed, q, other)
            c16, sums = gate_sums(i, q, u)
            y_next, u_next = project(i + 1, q, other)
            mixed_next = recur(i, q, y, c16, sums)
            kept(2, slot, q)[:] = mixed_next
            kept(0, other, q)[:] = y_next
            kept(1, other, q)[:] = u_next

        @pl.when(core == 0)
        def _():
            msg_out[i, :EDGE, :] = tail_s[:]
            msg_out[i, EDGE:, :] = h0_s[:]
            message(i).start()

        wait(back_tiles(i, slot))

        for g in range(1, blocks):
            @pl.when(i == 2 * g - 2)
            def _(g=g):
                @pl.when(core == 0)
                def _():
                    if g == 1:
                        forward(g, first(g))
                    relay(g, first(g))

                ready(g, first(g))
                start(in_tiles(i + 2, slot))

    ready(blocks, second(0))
    start(up_tiles(0, 0))

    @pl.loop(0, steps)
    def _(c):
        project_back(kept(2, (halves - 1) % 2, c)[:], c, (halves - 1) % 2)
        rows = part_of(c, CHUNK)
        vals = acc_s[rows, :]
        scale = lax.rsqrt(jnp.mean(vals * vals, axis=1, keepdims=True) + EPS)
        n_s[rows, :] = (vals * scale * (1.0 + wide(2))).astype(BF16)
        acc_s[rows, :] = vals + wide(3)

    def rows_of(i):
        return part_of(i, UP)

    def up(i, slot, b):
        vals = n_s[rows_of(i), :]
        for c in range(NCH):
            part = slice(c * model, (c + 1) * model)
            gate = jnp.dot(vals, t_w[slot, part], preferred_element_type=F32) + inner_row(c, 0, b)
            upper = jnp.dot(vals, t_w[2 + slot, part], preferred_element_type=F32) + inner_row(c, 1, b)
            act_s[c, rows_of(i), cols_of(b)] = (gelu(gate) * upper).astype(BF16)

    def ahead(s):
        return jnp.minimum(4 + s - (s > 4).astype(jnp.int32) - (s > 7).astype(jnp.int32), groups)

    @pl.loop(0, groups)
    def _(s):
        slot = lax.rem(s, 2)
        pass_on(ahead(s), ahead(s + 1))

        @pl.when(s == 9)
        def _():
            for d in range(DOWN):
                for kind in both:
                    down_piece(kind, d).start()

        wait(up_tiles(s, slot))

        @pl.loop(0, ups)
        def _(i):
            @pl.when((i == 1) & (s + 1 < groups))
            def _():
                relay(blocks + s + 1, second(s + 1))

            @pl.when((i == 3) & (s + 1 < groups))
            def _():
                ready(blocks + s + 1, second(s + 1))
                start(up_tiles(s + 1, 1 - slot))

            up(i, slot, s)

    base = me * tokens

    def col_block(b):
        return lax.rem(wd + lax.rem(b, 2) * (1 - 2 * core) + 2 * (b // 2) + NWD, NWD)

    def wide_cols(b):
        return wide_of(col_block(b))

    def across(i):
        return remote(n_s.at[rows_of(i), wide_cols(0)], out.at[pl.ds(base + i * UP, UP)], dev_y, fssem.at[0, i], frsem.at[0, i])

    def keep(i):
        return pltpu.make_async_copy(n_s.at[rows_of(i), wide_cols(0)], out.at[pl.ds(base + i * UP, UP)], olsem.at[i])

    def direct(b, i):
        return remote(n_s.at[rows_of(i), wide_cols(b)], out.at[pl.ds(base + i * UP, UP)], (0, ch, col_block(b)),
                      ossem.at[b - 1, i], orsem.at[b - 1, i])

    def onward(b, i):
        here = pl.ds((ch * NWD + col_block(b)) * tokens + i * UP, UP)
        return remote(out.at[here], out.at[here], dev_y, fssem.at[b, i], frsem.at[b, i])

    def load_down(b, p):
        side = lax.rem(ch + p // DOWN, NCH)
        rows = part_of(lax.rem(p, DOWN), deep)
        for half in range(2):
            cols = pl.ds(pl.multiple_of(col_block(b) * width + half * LANES, LANES), LANES)
            buf = t_w.at[p, pl.ds(half * deep, deep)]
            mine = (b == 0) & (p < DOWN)

            @pl.when(mine)
            def _():
                pltpu.make_async_copy(w_d.at[rows, cols_of(half)], buf, osem.at[p, half]).start()

            @pl.when(jnp.logical_not(mine))
            def _():
                pltpu.make_async_copy(g_d.at[side, rows, cols], buf, osem.at[p, half]).start()

    def wait_down(p):
        for half in range(2):
            pltpu.make_async_copy(w_d.at[pl.ds(0, deep), cols_of(half)], t_w.at[p, pl.ds(half * deep, deep)], osem.at[p, half]).wait()

    def down(b, p, i):
        side = lax.rem(ch + p // DOWN, NCH)
        vals = act_s[side, rows_of(i), part_of(lax.rem(p, DOWN), deep)]
        both = [jnp.dot(vals, t_w[p, half * deep:(half + 1) * deep], preferred_element_type=F32) for half in range(2)]
        acc_s[rows_of(i), wide_cols(b)] += jnp.concatenate(both, axis=1)

    def next_piece(b, p):
        d = lax.rem(p, DOWN)
        near = p < DOWN
        for at, kind_near, kind_far in ((0, OWN_P, Y_P), (1, None, Y_X), (2, X_P, D_P)):
            if kind_near is not None:
                @pl.when((b == at) & near)
                def _(kind=kind_near):
                    down_piece(kind, d).wait_recv()

            @pl.when((b == at) & jnp.logical_not(near))
            def _(kind=kind_far):
                down_piece(kind, d).wait_recv()
                if kind == Y_X:
                    down_piece(D_P, d).start()

        @pl.when(b < NWD - 1)
        def _():
            load_down(b + 1, p)

    def hand_out(b, i):
        back = shuffle_matrix(True)
        for c in range(UP // CHUNK):
            rows = pl.ds(i * UP + c * CHUNK, CHUNK)
            n_s[rows, wide_cols(b)] = jnp.dot(back, acc_s[rows, wide_cols(b)].astype(BF16), preferred_element_type=F32).astype(BF16)

        @pl.when(b == 0)
        def _():
            across(i).start()
            keep(i).start()

        @pl.when(b > 0)
        def _():
            direct(b, i).start()

    load_down(0, 0)
    load_down(0, 1)

    @pl.loop(0, NWD)
    def _(b):
        @pl.loop(0, 2 * DOWN)
        def _(p):
            @pl.when((b == 0) & (p >= DOWN))
            def _():
                forward_down(p - DOWN)
                load_down(0, p)

            wait_down(p)

            @pl.loop(0, ups)
            def _(i):
                down(b, p, i)

                @pl.when(p == 2 * DOWN - 1)
                def _():
                    hand_out(b, i)

            @pl.when((b == 1) & (p == 2 * DOWN - 1))
            def _():
                for i in range(ups):
                    direct(1, i).wait_recv()
                    onward(1, i).start()

            next_piece(b, p)

    for b in (2, 3):
        for i in range(ups):
            direct(b, i).wait_recv()
            onward(b, i).start()
    for g in range(blocks):
        drain(g, first(g))

    @pl.loop(0, groups)
    def _(b):
        drain(blocks + b, second(b))

    for d in range(DOWN):
        for kind in (OWN_X, OWN_Y, OWN_P, X_P, Y_P, Y_X, D_P):
            down_piece(kind, d).wait_send()
    by_core(lambda which: gate_over(which).wait_send())
    for q in range(NX):
        for p in (1, 2, 3):
            x_copy(p, q).wait_send()

    @pl.when(core == 0)
    def _():
        @pl.loop(0, halves)
        def _(i):
            message(i).wait_send()

    for i in range(ups):
        keep(i).wait()
        across(i).wait()
        for b in (1, 2, 3):
            direct(b, i).wait_send()
            onward(b, i).wait()


def solution(mesh):
    row_spec = P("dp", "wd")
    specs = (row_spec, P("dp"), P("wd"), P("wd", "ch"), P("ch"), P("wd", "ch"), P("ch"), P(None, "ch"), P("ch"), P("ch"), P("ch"), P("ch"), P("ch"), P("ch"), P("ch", "wd"), P("wd"), P("wd"), P("wd", "ch"), P("ch"), P("wd", "ch"), P("ch"), P("ch", "wd"), P("wd"))

    def local_layer(resid_in, seg_pos, gain_temporal, w_x, bias_x, w_y, bias_y, conv_w, conv_bias, lam_param, rgate_w, rgate_b, igate_w, igate_b, w_o, bias_o, gain_mlp, w_g, bias_g, w_u, bias_u, w_d, bias_d):
        tokens, width = resid_in.shape
        model = width * NWD
        rows = tokens // NDEV
        blocks = w_x.shape[1] // LANES
        groups = w_g.shape[1] // LANES
        total = NCH * blocks
        vectors = [bias_x, bias_y, conv_bias, conv_w.reshape(-1), -8.0 * jax.nn.softplus(-lam_param), rgate_b, igate_b, bias_g, bias_u,
                   gain_temporal, bias_o, gain_mlp, bias_d]
        flat = jnp.concatenate([v.astype(F32) for v in vectors])
        shared = (10 * blocks + 2 * groups) * LANES
        tail = flat.shape[0] - shared
        lead = -(-shared // 1024) * 1024
        small = jnp.concatenate([flat[:shared], jnp.zeros((lead - shared,), F32), jnp.zeros((-(-tail // 1024) * 1024 - tail,), F32), flat[shared:]]).reshape(-1, ROW)

        def like(w, by_rows):
            return jax.ShapeDtypeStruct((NCH, w.shape[0] * (1 if by_rows else NWD), w.shape[1] * (NWD if by_rows else 1)), BF16)

        dma = pltpu.SemaphoreType.DMA
        ups = rows // UP
        kinds = (8, blocks + groups, 3)
        outs = pl.pallas_call(
            layer,
            out_shape=[jax.ShapeDtypeStruct((tokens, width), BF16), like(w_y, False), like(w_x, False), like(w_o, True), like(w_g, False), like(w_u, False), like(w_d, True),
                       jax.ShapeDtypeStruct((rows, model), BF16)],
            in_specs=[ANY, pl.BlockSpec(memory_space=pltpu.VMEM)] + [ANY] * 9,
            out_specs=[ANY] * 8,
            scratch_shapes=[pltpu.VMEM((rows, model), BF16), pltpu.VMEM((rows, model), F32),
                            pltpu.VMEM((NCH, rows, w_g.shape[1]), BF16), pltpu.VMEM((4, NCH * model, LANES), BF16),
                            pltpu.VMEM((NCH, lead // ROW, ROW), F32), pltpu.VMEM((NWD, small.shape[0] - lead // ROW, ROW), F32), pltpu.VMEM((rows, ROW), jnp.int32),
                            pltpu.VMEM((CHUNK + EDGE, LANES), F32), pltpu.VMEM((CHUNK, LANES), F32), pltpu.VMEM((CHUNK, LANES), F32),
                            pltpu.VMEM((EDGE, LANES), F32), pltpu.VMEM((SUB, LANES), F32),
                            pltpu.VMEM((total, EDGE + SUB, LANES), F32), pltpu.VMEM((total, EDGE + SUB, LANES), F32),
                            dma(kinds), dma(kinds), dma((8, DOWN)), dma((8, DOWN)), dma((3, 2, NCH)), dma((2 * DOWN, 2)), dma((3, NX)), dma((3, NX)), dma((7,)), dma((7,)), dma((15,)),
                            dma((total,)), dma((total,)), dma((NWD,)), dma((3, ups)), dma((3, ups)), dma((4, ups)), dma((4, ups)), dma((ups,))],
            compiler_params=pltpu.CompilerParams(has_side_effects=True, vmem_limit_bytes=VMEM_LIMIT),
            name="layer",
        )(resid_in, seg_pos, w_y, w_x, w_o, w_g, w_u, w_d, rgate_w.reshape(-1, LANES), igate_w.reshape(-1, LANES), small)
        return outs[0]

    return jax.shard_map(local_layer, mesh=mesh, in_specs=specs, out_specs=row_spec, check_vma=False)
```

profile of v0, /device:TPU:0, one launch (start us, length us, event | category | flops | bytes accessed | tf_op | source)
XLA Modules:
  0.0 688.1 jit_solution(4626950922297602817)
XLA Ops:
  0.0 0.7 reshape.15
  0.7 0.7 convert_dynamic-update-slice_fusion.6
  1.4 0.7 convert_dynamic-update-slice_fusion.5
  2.1 0.7 convert_dynamic-update-slice_fusion.4
  2.8 0.7 fusion.1
  3.5 0.7 convert_dynamic-update-slice_fusion.3
  4.2 0.7 convert_dynamic-update-slice_fusion.2
  4.9 0.7 convert_dynamic-update-slice_fusion.1
  5.6 0.7 convert_dynamic-update-slice_fusion
  6.3 0.7 constant_dynamic-update-slice_fusion.3
  7.0 0.7 constant_dynamic-update-slice_fusion.2
  7.7 0.7 constant_dynamic-update-slice_fusion.1
  8.4 0.7 constant_dynamic-update-slice_fusion
  9.1 0.0 copy-start
  9.1 0.6 copy-done
  9.7 664.6 %layer.1 = (bf16[16384,512]{1,0:T(8,128)(2,1)}, bf16[2,2048,1280]{2,1,0:T(8,128)(2,1)}, bf16[2,2048,1280]{2,1,0:T(8,128)(2,1)}, bf16[2,1280,2048]{2,1,0:T(8,128)...) custom-call(bf16[16384,512]{1,0:T(8,128)(2,1)} %resid.1, ...), custom_call_target="tpu_custom_call" | custom-call | tf_op jit(solution)/shard_map/layer/pallas_call | solution.py:704
  674.3 13.8 %copy.39 = bf16[16384,512]{1,0:T(8,128)(2,1)} copy(bf16[16384,512]{1,0:T(8,128)(2,1)} %get-tuple-element.6) | data formatting | bytes 33554432
  (3 shorter events, 0.0 us)
Async XLA Ops:
  9.1 0.6 copy-start
where the time goes:
time: 689 us; the launch traced here: 688 us
  Pallas kernels  665 us (97%)
  local copies, waits for them, and re-layouts  15.1 us (2%)
  other arithmetic  8.32 us (1%)
    pallas_call x1, Pallas kernels, local_layer(): pl.pallas_call(layer, out_shape=[jax.ShapeDtypeStruct((tokens, width), BF...  665 us
    unnamed x5, local copies, waits for them, and re-layouts  14.4 us

commit v1 on v0

--- a/solution.py
+++ b/solution.py
@@ -156,8 +156,6 @@
         down_piece(OWN_Y, d).wait_recv()
         down_piece(Y_X, d).start()
         down_piece(Y_P, d).start()
-        down_piece(OWN_X, d).wait_recv()
-        down_piece(X_P, d).start()
 
     def in_tiles(j, slot):
         jj, side = j // NCH, lax.rem(j, NCH)
@@ -183,6 +181,7 @@
     send(0, first(0), both)
     shared = par_s.shape[1]
     tail_rows = pl.ds(small.shape[0] - vwd_s.shape[1], vwd_s.shape[1])
+    send(1, first(1), (OWN_Y, OWN_P))
     small_sends = [remote(small.at[pl.ds(0, shared)], par_s.at[ch], dev_y, pssem.at[0], prsem.at[0])]
     for p in (1, 2, 3):
         small_sends.append(remote(small.at[tail_rows], vwd_s.at[wd], (0, ch, lax.rem(wd + p, NWD)), pssem.at[p], prsem.at[p]))
@@ -230,10 +229,9 @@
             def _(which=which):
                 do(which)
 
-    for g in range(1, blocks):
+    by_core(lambda which: gate_over(which).start())
+    for g in range(2, blocks):
         send(g, first(g), (OWN_Y, OWN_P))
-        if g == 1:
-            by_core(lambda which: gate_over(which).start())
     send(blocks, second(0), both)
     send(blocks + 1, second(1), (OWN_X,))
     send(blocks + 2, second(2), (OWN_X,))
@@ -396,15 +394,6 @@
 
         pass_on(came(i + core), came(i + core + 1))
 
-        def onward_first(of):
-            for at, g in ((1, 2), (2, 3), (3, 4)):
-                @pl.when((core == of) & (i == at))
-                def _(at=at, g=g):
-                    forward(g, first(g))
-                    if at > 1:
-                        send(blocks + at - 1, second(at - 1), (OWN_Y, OWN_P))
-
-        onward_first(1)
         for g, at in ((1, 0), (2, 2), (3, 4), (4, 6)):
             @pl.when((core == 1) & (i == at))
             def _(g=g):
@@ -416,6 +405,13 @@
         def _():
             relay(blocks, second(0))
 
+        for g in range(2, blocks):
+            @pl.when(i + core == g - 1)
+            def _(g=g):
+                forward(g, first(g))
+                if g > 2:
+                    send(blocks + g - 2, second(g - 2), (OWN_Y, OWN_P))
+
         @pl.when(i < halves - 1)
         def _():
             wait(in_tiles(i + 1, other))
@@ -427,8 +423,6 @@
         start(back_tiles(i, slot))
 
         def middle():
-            onward_first(0)
-
             @pl.when((core == 0) & (i == 8))
             def _():
                 relay(blocks, second(0))
@@ -479,6 +473,7 @@
                 ready(g, first(g))
                 start(in_tiles(i + 2, slot))
 
+    pass_on(4, 5)
     ready(blocks, second(0))
     start(up_tiles(0, 0))
 
@@ -503,18 +498,19 @@
             act_s[c, rows_of(i), cols_of(b)] = (gelu(gate) * upper).astype(BF16)
 
     def ahead(s):
-        return jnp.minimum(4 + s - (s > 4).astype(jnp.int32) - (s > 7).astype(jnp.int32), groups)
+        return jnp.minimum(5 + s - (s > 5).astype(jnp.int32) - (s > 7).astype(jnp.int32), groups)
 
     @pl.loop(0, groups)
     def _(s):
         slot = lax.rem(s, 2)
         pass_on(ahead(s), ahead(s + 1))
 
-        @pl.when(s == 9)
-        def _():
-            for d in range(DOWN):
-                for kind in both:
-                    down_piece(kind, d).start()
+        for at, kinds, low, high in ((6, (OWN_Y, OWN_P), 0, 1), (8, (OWN_Y, OWN_P), 1, DOWN), (8, (OWN_X,), 0, DOWN)):
+            @pl.when(s == at)
+            def _(kinds=kinds, low=low, high=high):
+                for d in range(low, high):
+                    for kind in kinds:
+                        down_piece(kind, d).start()
 
         wait(up_tiles(s, slot))
 
@@ -539,19 +535,24 @@
     def wide_cols(b):
         return wide_of(col_block(b))
 
-    def across(i):
-        return remote(n_s.at[rows_of(i), wide_cols(0)], out.at[pl.ds(base + i * UP, UP)], dev_y, fssem.at[0, i], frsem.at[0, i])
-
-    def keep(i):
-        return pltpu.make_async_copy(n_s.at[rows_of(i), wide_cols(0)], out.at[pl.ds(base + i * UP, UP)], olsem.at[i])
-
-    def direct(b, i):
-        return remote(n_s.at[rows_of(i), wide_cols(b)], out.at[pl.ds(base + i * UP, UP)], (0, ch, col_block(b)),
-                      ossem.at[b - 1, i], orsem.at[b - 1, i])
-
-    def onward(b, i):
-        here = pl.ds((ch * NWD + col_block(b)) * tokens + i * UP, UP)
-        return remote(out.at[here], out.at[here], dev_y, fssem.at[b, i], frsem.at[b, i])
+    def there(q):
+        return part_of(q, CHUNK), out.at[pl.ds(base + q * CHUNK, CHUNK)]
+
+    def across(q):
+        rows, place = there(q)
+        return remote(n_s.at[rows, wide_cols(0)], place, dev_y, fssem.at[0, q], frsem.at[0, q])
+
+    def keep(q):
+        rows, place = there(q)
+        return pltpu.make_async_copy(n_s.at[rows, wide_cols(0)], place, olsem.at[q])
+
+    def direct(b, q):
+        rows, place = there(q)
+        return remote(n_s.at[rows, wide_cols(b)], place, (0, ch, col_block(b)), ossem.at[b - 1, q], orsem.at[b - 1, q])
+
+    def onward(b, q):
+        here = out.at[pl.ds((ch * NWD + col_block(b)) * tokens + q * CHUNK, CHUNK)]
+        return remote(here, here, dev_y, fssem.at[b, q], frsem.at[b, q])
 
     def load_down(b, p):
         side = lax.rem(ch + p // DOWN, NCH)
@@ -582,17 +583,13 @@
     def next_piece(b, p):
         d = lax.rem(p, DOWN)
         near = p < DOWN
-        for at, kind_near, kind_far in ((0, OWN_P, Y_P), (1, None, Y_X), (2, X_P, D_P)):
-            if kind_near is not None:
-                @pl.when((b == at) & near)
-                def _(kind=kind_near):
+        for at, kind_near, kind_far in ((0, OWN_P, Y_P), (1, OWN_X, Y_X), (2, X_P, D_P)):
+            for kind, here in ((kind_near, near), (kind_far, jnp.logical_not(near))):
+                @pl.when((b == at) & here)
+                def _(kind=kind):
                     down_piece(kind, d).wait_recv()
-
-            @pl.when((b == at) & jnp.logical_not(near))
-            def _(kind=kind_far):
-                down_piece(kind, d).wait_recv()
-                if kind == Y_X:
-                    down_piece(D_P, d).start()
+                    if kind in (OWN_X, Y_X):
+                        down_piece(X_P if kind == OWN_X else D_P, d).start()
 
         @pl.when(b < NWD - 1)
         def _():
@@ -601,17 +598,24 @@
     def hand_out(b, i):
         back = shuffle_matrix(True)
         for c in range(UP // CHUNK):
-            rows = pl.ds(i * UP + c * CHUNK, CHUNK)
+            q = i * (UP // CHUNK) + c
+            rows = part_of(q, CHUNK)
             n_s[rows, wide_cols(b)] = jnp.dot(back, acc_s[rows, wide_cols(b)].astype(BF16), preferred_element_type=F32).astype(BF16)
 
-        @pl.when(b == 0)
-        def _():
-            across(i).start()
-            keep(i).start()
-
-        @pl.when(b > 0)
-        def _():
-            direct(b, i).start()
+            @pl.when(b == 0)
+            def _():
+                across(q).start()
+                keep(q).start()
+
+            @pl.when(b > 0)
+            def _():
+                direct(b, q).start()
+
+    def pass_results(b, low, high):
+        @pl.loop(low, high)
+        def _(q):
+            direct(b, q).wait_recv()
+            onward(b, q).start()
 
     load_down(0, 0)
     load_down(0, 1)
@@ -635,18 +639,28 @@
                 def _():
                     hand_out(b, i)
 
+            @pl.when(b != 1)
+            def _():
+                next_piece(b, p)
+
             @pl.when((b == 1) & (p == 2 * DOWN - 1))
             def _():
-                for i in range(ups):
-                    direct(1, i).wait_recv()
-                    onward(1, i).start()
-
-            next_piece(b, p)
-
-    for b in (2, 3):
-        for i in range(ups):
-            direct(b, i).wait_recv()
-            onward(b, i).start()
+                pass_results(b, 0, steps)
+
+                @pl.loop(0, p)
+                def _(k):
+                    next_piece(b, k)
+
+            @pl.when((b == NWD - 1) & (p < DOWN))
+            def _():
+                pass_results(2, p * 2, p * 2 + 2)
+
+            @pl.when((b == 2) & (p == 2 * DOWN - 2))
+            def _():
+                next_piece(b - 1, p + 1)
+
+    pass_results(2, 2 * DOWN, steps)
+    pass_results(3, 0, steps)
     for g in range(blocks):
         drain(g, first(g))
 
@@ -668,12 +682,13 @@
         def _(i):
             message(i).wait_send()
 
-    for i in range(ups):
-        keep(i).wait()
-        across(i).wait()
-        for b in (1, 2, 3):
-            direct(b, i).wait_send()
-            onward(b, i).wait()
+    @pl.loop(0, steps)
+    def _(q):
+        keep(q).wait()
+        across(q).wait()
+        for b in range(1, NWD):
+            direct(b, q).wait_send()
+            onward(b, q).wait()
 
 
 def solution(mesh):
@@ -687,19 +702,23 @@
         blocks = w_x.shape[1] // LANES
         groups = w_g.shape[1] // LANES
         total = NCH * blocks
-        vectors = [bias_x, bias_y, conv_bias, conv_w.reshape(-1), -8.0 * jax.nn.softplus(-lam_param), rgate_b, igate_b, bias_g, bias_u,
+        vectors = [bias_x, bias_y, conv_bias, *conv_w, -8.0 * jax.nn.softplus(-lam_param), rgate_b, igate_b, bias_g, bias_u,
                    gain_temporal, bias_o, gain_mlp, bias_d]
-        flat = jnp.concatenate([v.astype(F32) for v in vectors])
         shared = (10 * blocks + 2 * groups) * LANES
-        tail = flat.shape[0] - shared
         lead = -(-shared // 1024) * 1024
-        small = jnp.concatenate([flat[:shared], jnp.zeros((lead - shared,), F32), jnp.zeros((-(-tail // 1024) * 1024 - tail,), F32), flat[shared:]]).reshape(-1, ROW)
+        whole = lead + 4 * width
+        at, packed = 0, jnp.zeros((whole,), F32)
+        for v in vectors:
+            at = lead if at == shared else at
+            packed = packed + lax.pad(v.astype(F32), jnp.zeros((), F32), [(at, whole - at - v.shape[0], 0)])
+            at += v.shape[0]
+        small = packed.reshape(-1, ROW)
 
         def like(w, by_rows):
             return jax.ShapeDtypeStruct((NCH, w.shape[0] * (1 if by_rows else NWD), w.shape[1] * (NWD if by_rows else 1)), BF16)
 
         dma = pltpu.SemaphoreType.DMA
-        ups = rows // UP
+        steps = rows // CHUNK
         kinds = (8, blocks + groups, 3)
         outs = pl.pallas_call(
             layer,
@@ -714,7 +733,7 @@
                             pltpu.VMEM((EDGE, LANES), F32), pltpu.VMEM((SUB, LANES), F32),
                             pltpu.VMEM((total, EDGE + SUB, LANES), F32), pltpu.VMEM((total, EDGE + SUB, LANES), F32),
                             dma(kinds), dma(kinds), dma((8, DOWN)), dma((8, DOWN)), dma((3, 2, NCH)), dma((2 * DOWN, 2)), dma((3, NX)), dma((3, NX)), dma((7,)), dma((7,)), dma((15,)),
-                            dma((total,)), dma((total,)), dma((NWD,)), dma((3, ups)), dma((3, ups)), dma((4, ups)), dma((4, ups)), dma((ups,))],
+                            dma((total,)), dma((total,)), dma((NWD,)), dma((3, steps)), dma((3, steps)), dma((4, steps)), dma((4, steps)), dma((steps,))],
             compiler_params=pltpu.CompilerParams(has_side_effects=True, vmem_limit_bytes=VMEM_LIMIT),
             name="layer",
         )(resid_in, seg_pos, w_y, w_x, w_o, w_g, w_u, w_d, rgate_w.reshape(-1, LANES), igate_w.reshape(-1, LANES), small)

time: 689 us -> 665 us (0.965)
  Pallas kernels: 665 us -> 648 us
    pallas_call x1, Pallas kernels: 665 us -> 648 us  [local_layer(): pl.pallas_call(layer, out_shape=[jax.ShapeDtypeStruct((tokens, width), BF...]
    unnamed x12 -> x0, other arithmetic: 7.64 us -> none
    unnamed x5 -> x1, local copies, waits for them, and re-layouts: 14.4 us -> 13.8 us
where the time goes in v1:
time: 665 us; the launch traced here: 664 us
  Pallas kernels  648 us (97%)
  local copies, waits for them, and re-layouts  14.7 us (2%)
    pallas_call x1, Pallas kernels, local_layer(): pl.pallas_call(layer, out_shape=[jax.ShapeDtypeStruct((tokens, width), BF...  648 us
    unnamed x1, local copies, waits for them, and re-layouts  13.8 us

profile of v1, /device:TPU:0, one launch (start us, length us, event | category | flops | bytes accessed | tf_op | source)
XLA Modules:
  0.0 664.5 jit_solution(3106814225856180457)
XLA Ops:
  0.0 0.7 fusion
  0.7 0.9 slice_reduce_fusion.3
  1.6 1.5 add_bitcast_fusion.small
  3.1 647.5 %layer.1 = (bf16[16384,512]{1,0:T(8,128)(2,1)}, bf16[2,2048,1280]{2,1,0:T(8,128)(2,1)}, bf16[2,2048,1280]{2,1,0:T(8,128)(2,1)}, bf16[2,1280,2048]{2,1,0:T(8,128)...) custom-call(bf16[16384,512]{1,0:T(8,128)(2,1)} %resid.1, ...), custom_call_target="tpu_custom_call" | custom-call | tf_op jit(solution)/shard_map/layer/pallas_call | solution.py:723
  650.7 13.8 %copy.25 = bf16[16384,512]{1,0:T(8,128)(2,1)} copy(bf16[16384,512]{1,0:T(8,128)(2,1)} %get-tuple-element.6) | data formatting | bytes 33554432

commit v2 on v1

--- a/solution.py
+++ b/solution.py
@@ -43,10 +43,11 @@
     return jnp.where((out % SUB) * (CHUNK // SUB) + out // SUB == src, 1.0, 0.0).astype(BF16)
 
 
-def layer(resid, seg_ref, w_y, w_x, w_o, w_g, w_u, w_d, rgate, igate, small,
+def layer(resid, seg_ref, w_y, w_x, w_o, w_g, w_u, w_d, rgate, igate, bias_x, bias_y, conv_bias, conv_w, lam_param, rgate_b, igate_b, bias_g, bias_u,
+          gain_temporal, bias_o, gain_mlp, bias_d,
           out, g_y, g_x, g_o, g_g, g_u, g_d, x_far,
-          n_s, acc_s, act_s, t_w, par_s, vwd_s, pos_s, u_s, h_s, prod_s, tail_s, h0_s,
-          msg_out, msg_in, ssem, rsem, dssem, drsem, tsem, osem, xssem, xrsem, pssem, prsem, lsem, mssem, mrsem, xlsem, ossem, orsem, fssem, frsem, olsem):
+          v_conv, v_lam, v_chan, v_inner, v_model, n_s, acc_s, act_s, t_w, par_s, vwd_s, pos_s, u_s, h_s, prod_s, tail_s, h0_s,
+          msg_out, msg_in, ssem, rsem, dssem, drsem, tsem, osem, vsem, xssem, xrsem, pssem, prsem, lsem, mssem, mrsem, xlsem, ossem, orsem, fssem, frsem, olsem):
     ch, wd = lax.axis_index("ch"), lax.axis_index("wd")
     core = lax.rem(wd, 2)
     me = ch * NWD + wd
@@ -178,17 +179,37 @@
         for d in copies:
             d.wait()
 
+    barrier = pltpu.get_barrier_semaphore()
+    peers = (dev_x, dev_y, dev_p, (0, ch, lax.rem(wp + 2, NWD)))
+    for device in peers:
+        pl.semaphore_signal(barrier, device_id=device, device_id_type=MESH)
+    pl.semaphore_wait(barrier, len(peers))
+
     send(0, first(0), both)
-    shared = par_s.shape[1]
-    tail_rows = pl.ds(small.shape[0] - vwd_s.shape[1], vwd_s.shape[1])
     send(1, first(1), (OWN_Y, OWN_P))
-    small_sends = [remote(small.at[pl.ds(0, shared)], par_s.at[ch], dev_y, pssem.at[0], prsem.at[0])]
+    chan_vectors = (bias_x, bias_y, conv_bias, rgate_b, igate_b)
+    loads = [*zip(chan_vectors, v_chan), (conv_w, v_conv), (lam_param, v_lam), *zip((bias_g, bias_u), v_inner),
+             *zip((gain_temporal, bias_o, gain_mlp, bias_d), v_model)]
+    small_loads = [pltpu.make_async_copy(v, d, vsem.at[i]) for i, (v, d) in enumerate(loads)]
+    small_own = [pltpu.make_async_copy(s, d, lsem.at[i]) for i, (s, d) in enumerate([(rgate, gate_area(0, ch)), (igate, gate_area(1, ch))])]
+    start(small_loads)
+    start(small_own)
+
+    wait(small_loads)
+    at = 0
+    chan = [v[:] for v in v_chan]
+    decay = -8.0 * jax.nn.softplus(-v_lam[:])
+    for v in chan[:3] + [v_conv[k] for k in range(conv_w.shape[0])] + [decay] + chan[3:] + [v[:] for v in v_inner]:
+        count = v.shape[0] // ROW
+        par_s[ch, at:at + count, :] = v.astype(F32).reshape(count, ROW)
+        at += count
+    per = width // ROW
+    for i, v in enumerate(v_model):
+        vwd_s[wd, i * per:(i + 1) * per, :] = v[:].astype(F32).reshape(per, ROW)
+    small_sends = [remote(par_s.at[ch], par_s.at[ch], dev_y, pssem.at[0], prsem.at[0])]
     for p in (1, 2, 3):
-        small_sends.append(remote(small.at[tail_rows], vwd_s.at[wd], (0, ch, lax.rem(wd + p, NWD)), pssem.at[p], prsem.at[p]))
-    small_own = [pltpu.make_async_copy(s, d, lsem.at[i]) for i, (s, d) in enumerate(
-        [(small.at[pl.ds(0, shared)], par_s.at[ch]), (small.at[tail_rows], vwd_s.at[wd]), (rgate, gate_area(0, ch)), (igate, gate_area(1, ch))])]
+        small_sends.append(remote(vwd_s.at[wd], vwd_s.at[wd], (0, ch, lax.rem(wd + p, NWD)), pssem.at[p], prsem.at[p]))
     start(small_sends)
-    start(small_own)
 
     tall = w_y.shape[1]
     stay = [(w_y, act_s.at[0, pl.ds(0, width), pl.ds(0, tall)], g_y.at[ch, wide_of(wd)]),
@@ -242,9 +263,7 @@
     start(in_tiles(1, 1))
 
     def wide(i):
-        per = width // ROW
-        first_row = vwd_s.shape[1] - 4 * per + i * per
-        return jnp.concatenate([vwd_s[k, first_row + r:first_row + r + 1, :] for k in range(NWD) for r in range(per)], axis=1)
+        return jnp.concatenate([vwd_s[k, i * per + r:i * per + r + 1, :] for k in range(NWD) for r in range(per)], axis=1)
 
     def narrow(side, base, i):
         return jnp.concatenate([par_s[side, pl.ds(base + 2 * i + r, 1), :] for r in range(2)], axis=1)
@@ -691,6 +710,19 @@
             onward(b, q).wait()
 
 
+def put_out(src, dst, buf, isem, osem):
+    part = src.shape[0] // SUB
+    ins = [pltpu.make_async_copy(src.at[pl.ds(k * part, part)], buf.at[pl.ds(k * part, part)], isem.at[k]) for k in range(SUB)]
+    outs = [pltpu.make_async_copy(buf.at[pl.ds(k * part, part)], dst.at[pl.ds(k * part, part)], osem.at[k]) for k in range(SUB)]
+    for c in ins:
+        c.start()
+    for c, d in zip(ins, outs):
+        c.wait()
+        d.start()
+    for d in outs:
+        d.wait()
+
+
 def solution(mesh):
     row_spec = P("dp", "wd")
     specs = (row_spec, P("dp"), P("wd"), P("wd", "ch"), P("ch"), P("wd", "ch"), P("ch"), P(None, "ch"), P("ch"), P("ch"), P("ch"), P("ch"), P("ch"), P("ch"), P("ch", "wd"), P("wd"), P("wd"), P("wd", "ch"), P("ch"), P("wd", "ch"), P("ch"), P("ch", "wd"), P("wd"))
@@ -702,17 +734,10 @@
         blocks = w_x.shape[1] // LANES
         groups = w_g.shape[1] // LANES
         total = NCH * blocks
-        vectors = [bias_x, bias_y, conv_bias, *conv_w, -8.0 * jax.nn.softplus(-lam_param), rgate_b, igate_b, bias_g, bias_u,
-                   gain_temporal, bias_o, gain_mlp, bias_d]
-        shared = (10 * blocks + 2 * groups) * LANES
-        lead = -(-shared // 1024) * 1024
-        whole = lead + 4 * width
-        at, packed = 0, jnp.zeros((whole,), F32)
-        for v in vectors:
-            at = lead if at == shared else at
-            packed = packed + lax.pad(v.astype(F32), jnp.zeros((), F32), [(at, whole - at - v.shape[0], 0)])
-            at += v.shape[0]
-        small = packed.reshape(-1, ROW)
+        vectors = (bias_x, bias_y, conv_bias, conv_w, lam_param, rgate_b, igate_b, bias_g, bias_u, gain_temporal, bias_o, gain_mlp, bias_d)
+        chan, inner = w_x.shape[1], w_g.shape[1]
+        shared = (10 * chan + 2 * inner) // ROW
+        lead = -(-shared // SUB) * SUB
 
         def like(w, by_rows):
             return jax.ShapeDtypeStruct((NCH, w.shape[0] * (1 if by_rows else NWD), w.shape[1] * (NWD if by_rows else 1)), BF16)
@@ -724,19 +749,24 @@
             layer,
             out_shape=[jax.ShapeDtypeStruct((tokens, width), BF16), like(w_y, False), like(w_x, False), like(w_o, True), like(w_g, False), like(w_u, False), like(w_d, True),
                        jax.ShapeDtypeStruct((rows, model), BF16)],
-            in_specs=[ANY, pl.BlockSpec(memory_space=pltpu.VMEM)] + [ANY] * 9,
+            in_specs=[ANY, pl.BlockSpec(memory_space=pltpu.VMEM)] + [ANY] * (8 + len(vectors)),
             out_specs=[ANY] * 8,
-            scratch_shapes=[pltpu.VMEM((rows, model), BF16), pltpu.VMEM((rows, model), F32),
+            scratch_shapes=[pltpu.VMEM(conv_w.shape, BF16), pltpu.VMEM((chan,), F32), [pltpu.VMEM((chan,), BF16)] * 5, [pltpu.VMEM((inner,), BF16)] * 2, [pltpu.VMEM((width,), BF16)] * 4,
+                            pltpu.VMEM((rows, model), BF16), pltpu.VMEM((rows, model), F32),
                             pltpu.VMEM((NCH, rows, w_g.shape[1]), BF16), pltpu.VMEM((4, NCH * model, LANES), BF16),
-                            pltpu.VMEM((NCH, lead // ROW, ROW), F32), pltpu.VMEM((NWD, small.shape[0] - lead // ROW, ROW), F32), pltpu.VMEM((rows, ROW), jnp.int32),
+                            pltpu.VMEM((NCH, lead, ROW), F32), pltpu.VMEM((NWD, 4 * width // ROW, ROW), F32), pltpu.VMEM((rows, ROW), jnp.int32),
                             pltpu.VMEM((CHUNK + EDGE, LANES), F32), pltpu.VMEM((CHUNK, LANES), F32), pltpu.VMEM((CHUNK, LANES), F32),
                             pltpu.VMEM((EDGE, LANES), F32), pltpu.VMEM((SUB, LANES), F32),
                             pltpu.VMEM((total, EDGE + SUB, LANES), F32), pltpu.VMEM((total, EDGE + SUB, LANES), F32),
-                            dma(kinds), dma(kinds), dma((8, DOWN)), dma((8, DOWN)), dma((3, 2, NCH)), dma((2 * DOWN, 2)), dma((3, NX)), dma((3, NX)), dma((7,)), dma((7,)), dma((15,)),
+                            dma(kinds), dma(kinds), dma((8, DOWN)), dma((8, DOWN)), dma((3, 2, NCH)), dma((2 * DOWN, 2)), dma((len(vectors),)), dma((3, NX)), dma((3, NX)), dma((7,)), dma((7,)), dma((15,)),
                             dma((total,)), dma((total,)), dma((NWD,)), dma((3, steps)), dma((3, steps)), dma((4, steps)), dma((4, steps)), dma((steps,))],
-            compiler_params=pltpu.CompilerParams(has_side_effects=True, vmem_limit_bytes=VMEM_LIMIT),
+            compiler_params=pltpu.CompilerParams(collective_id=0, has_side_effects=True, vmem_limit_bytes=VMEM_LIMIT),
             name="layer",
-        )(resid_in, seg_pos, w_y, w_x, w_o, w_g, w_u, w_d, rgate_w.reshape(-1, LANES), igate_w.reshape(-1, LANES), small)
-        return outs[0]
+        )(resid_in, seg_pos, w_y, w_x, w_o, w_g, w_u, w_d, rgate_w.reshape(-1, LANES), igate_w.reshape(-1, LANES), *vectors)
+        return pl.pallas_call(
+            put_out, out_shape=jax.ShapeDtypeStruct((tokens, width), BF16), in_specs=[ANY], out_specs=ANY,
+            scratch_shapes=[pltpu.VMEM((tokens, width), BF16), dma((SUB,)), dma((SUB,))],
+            compiler_params=pltpu.CompilerParams(vmem_limit_bytes=VMEM_LIMIT), name="put_out",
+        )(outs[0])
 
     return jax.shard_map(local_layer, mesh=mesh, in_specs=specs, out_specs=row_spec, check_vma=False)

time: 665 us -> 659 us (level)
  local copies, waits for them, and re-layouts: 14.7 us -> 0 us
  Pallas kernels: 648 us -> 658 us
    unnamed x1 -> x0, local copies, waits for them, and re-layouts: 13.8 us -> none
    pallas_call x0 -> x1, Pallas kernels: none -> 11.8 us  [local_layer(): pl.pallas_call(put_out, out_shape=jax.ShapeDtypeStruct((tokens, width), B...]
where the time goes in v2:
time: 659 us; the launch traced here: 658 us
  Pallas kernels  658 us (100%)
    pallas_call x1, Pallas kernels, local_layer(): pl.pallas_call(layer, out_shape=[jax.ShapeDtypeStruct((tokens, width), BF...  646 us

profile of v2, /device:TPU:0, one launch (start us, length us, event | category | flops | bytes accessed | tf_op | source)
XLA Modules:
  0.0 658.1 jit_solution(12146950757082300419)
XLA Ops:
  0.0 646.3 %layer.1 = (bf16[16384,512]{1,0:T(8,128)(2,1)}, bf16[2,2048,1280]{2,1,0:T(8,128)(2,1)}, bf16[2,2048,1280]{2,1,0:T(8,128)(2,1)}, bf16[2,1280,2048]{2,1,0:T(8,128)...) custom-call(bf16[16384,512]{1,0:T(8,128)(2,1)} %resid.1, ...), custom_call_target="tpu_custom_call" | custom-call | tf_op jit(solution)/shard_map/layer/pallas_call | solution.py:748
  646.3 11.8 %put_out.1 = bf16[16384,512]{1,0:T(8,128)(2,1)} custom-call(bf16[16384,512]{1,0:T(8,128)(2,1)} %get-tuple-element.6.src), custom_call_target="tpu_custom_call" | custom-call | tf_op jit(solution)/shard_map/put_out/pallas_call | solution.py:766

commit v3 on v2

--- a/solution.py
+++ b/solution.py
@@ -15,7 +15,7 @@
 ROW = 128
 UP = 512
 DOWN = 2
-NEAR = 224
+NEAR = 216
 NX = 4
 NWD, NCH = 4, 2
 NDEV = NWD * NCH
@@ -100,7 +100,7 @@
         base, size = (0, width) if part is None else ((0, NEAR), (NEAR, width - NEAR))[part]
         if owner is None:
             return mine.at[pl.ds(base, size), cols_of(i)]
-        return far.at[owner[0], pl.ds(pl.multiple_of(owner[1] * width + base, 32), size), cols_of(i)]
+        return far.at[owner[0], pl.ds(pl.multiple_of(owner[1] * width + base, SUB), size), cols_of(i)]
 
     def transfer(kind, g, u, unit):
         split = not unit[-1] and unit[0] is not w_y and unit[0] is not w_x
@@ -517,19 +517,18 @@
             act_s[c, rows_of(i), cols_of(b)] = (gelu(gate) * upper).astype(BF16)
 
     def ahead(s):
-        return jnp.minimum(5 + s - (s > 5).astype(jnp.int32) - (s > 7).astype(jnp.int32), groups)
+        return jnp.minimum(5 + s - (s > 5).astype(jnp.int32), groups)
 
     @pl.loop(0, groups)
     def _(s):
         slot = lax.rem(s, 2)
         pass_on(ahead(s), ahead(s + 1))
 
-        for at, kinds, low, high in ((6, (OWN_Y, OWN_P), 0, 1), (8, (OWN_Y, OWN_P), 1, DOWN), (8, (OWN_X,), 0, DOWN)):
-            @pl.when(s == at)
-            def _(kinds=kinds, low=low, high=high):
-                for d in range(low, high):
-                    for kind in kinds:
-                        down_piece(kind, d).start()
+        @pl.when(s == 7)
+        def _():
+            for d in range(DOWN):
+                for kind in both:
+                    down_piece(kind, d).start()
 
         wait(up_tiles(s, slot))
 

time: 659 us -> 655 us (level)
  no operation moved by 1% of the time
where the time goes in v3:
time: 655 us
  Pallas kernels  655 us (100%)
    pallas_call x1, Pallas kernels, local_layer(): pl.pallas_call(layer, out_shape=[jax.ShapeDtypeStruct((tokens, width), BF...  643 us

profile of v3, /device:TPU:0, one launch (start us, length us, event | category | flops | bytes accessed | tf_op | source)
XLA Modules:
  0.0 654.9 jit_solution(370458325007674085)
XLA Ops:
  0.0 643.1 %layer.1 = (bf16[16384,512]{1,0:T(8,128)(2,1)}, bf16[2,2048,1280]{2,1,0:T(8,128)(2,1)}, bf16[2,2048,1280]{2,1,0:T(8,128)(2,1)}, bf16[2,1280,2048]{2,1,0:T(8,128)...) custom-call(bf16[16384,512]{1,0:T(8,128)(2,1)} %resid.1, ...), custom_call_target="tpu_custom_call" | custom-call | tf_op jit(solution)/shard_map/layer/pallas_call | solution.py:747
  643.1 11.8 %put_out.1 = bf16[16384,512]{1,0:T(8,128)(2,1)} custom-call(bf16[16384,512]{1,0:T(8,128)(2,1)} %get-tuple-element.6.src), custom_call_target="tpu_custom_call" | custom-call | tf_op jit(solution)/shard_map/put_out/pallas_call | solution.py:765

commit v4 on v3

--- a/solution.py
+++ b/solution.py
@@ -47,7 +47,7 @@
           gain_temporal, bias_o, gain_mlp, bias_d,
           out, g_y, g_x, g_o, g_g, g_u, g_d, x_far,
           v_conv, v_lam, v_chan, v_inner, v_model, n_s, acc_s, act_s, t_w, par_s, vwd_s, pos_s, u_s, h_s, prod_s, tail_s, h0_s,
-          msg_out, msg_in, ssem, rsem, dssem, drsem, tsem, osem, vsem, xssem, xrsem, pssem, prsem, lsem, mssem, mrsem, xlsem, ossem, orsem, fssem, frsem, olsem):
+          msg_out, msg_in, ssem, rsem_t, rsem_u, dssem, drsem, tsem, osem, vsem, xssem, xrsem, pssem, prsem, lsem, mssem, mrsem, xlsem, ossem, orsem, fssem, frsem, olsem):
     ch, wd = lax.axis_index("ch"), lax.axis_index("wd")
     core = lax.rem(wd, 2)
     me = ch * NWD + wd
@@ -107,7 +107,7 @@
         owner, part, device = {OWN_X: (None, None, dev_x), OWN_Y: (None, None, dev_y), OWN_P: (None, None, dev_p),
                                X_P: (far_x, None, dev_p), X_Y: (far_x, 0 if split else None, dev_y),
                                Y_P: (far_y, None, dev_p), Y_X: (far_y, 1, dev_x), D_P: (far_d, None, dev_p)}[kind]
-        return remote(cut(unit, owner, part), cut(unit, owner or own, part), device, ssem.at[kind, g, u], rsem.at[kind, g, u])
+        return remote(cut(unit, owner, part), cut(unit, owner or own, part), device, ssem.at[g], rsem_u.at[kind, g - blocks, u] if unit[0] is w_g or unit[0] is w_u else rsem_t.at[kind, g, u])
 
     def send(g, units, kinds):
         for kind in kinds:
@@ -137,11 +137,9 @@
             for kind in (OWN_P, X_P, Y_P, D_P):
                 transfer(kind, g, u, unit).wait_recv()
 
-    def drain(g, units):
-        for u, unit in enumerate(units):
-            for kind in range(8):
-                if len(units) == NCH or kind != Y_X:
-                    transfer(kind, g, u, unit).wait_send()
+    def sent(sem, *shape):
+        bytes_of_all = g_g.at[tuple(pl.ds(0, n) for n in shape)] if len(shape) > 2 else g_g.at[0, pl.ds(0, shape[0]), pl.ds(0, shape[1])]
+        remote(bytes_of_all, bytes_of_all, dev_y, sem, drsem.at[0, 0]).wait_send()
 
     both = (OWN_X, OWN_Y, OWN_P)
 
@@ -151,7 +149,7 @@
         rows = part_of(d, deep)
         at = owner or own
         far = g_d.at[at[0], rows, wide_of(at[1])]
-        return remote(w_d.at[rows] if owner is None else far, far, device, dssem.at[kind, d], drsem.at[kind, d])
+        return remote(w_d.at[rows] if owner is None else far, far, device, dssem.at[0], drsem.at[kind, d])
 
     def forward_down(d):
         down_piece(OWN_Y, d).wait_recv()
@@ -226,7 +224,7 @@
     def x_copy(p, q):
         peer = lax.rem(wd + p, NWD)
         return remote(resid.at[pl.ds((ch * NWD + peer) * tokens + q * rows_x, rows_x)], x_far.at[pl.ds(q * rows_x, rows_x), wide_of(wd)],
-                      (0, ch, peer), xssem.at[p - 1, q], xrsem.at[p - 1, q])
+                      (0, ch, peer), xssem.at[0], xrsem.at[p - 1, q])
 
     for q in range(NX):
         for p in (2, 1, 3):
@@ -558,7 +556,7 @@
 
     def across(q):
         rows, place = there(q)
-        return remote(n_s.at[rows, wide_cols(0)], place, dev_y, fssem.at[0, q], frsem.at[0, q])
+        return remote(n_s.at[rows, wide_cols(0)], place, dev_y, fssem.at[0], frsem.at[0, q])
 
     def keep(q):
         rows, place = there(q)
@@ -566,11 +564,11 @@
 
     def direct(b, q):
         rows, place = there(q)
-        return remote(n_s.at[rows, wide_cols(b)], place, (0, ch, col_block(b)), ossem.at[b - 1, q], orsem.at[b - 1, q])
+        return remote(n_s.at[rows, wide_cols(b)], place, (0, ch, col_block(b)), ossem.at[0], orsem.at[b - 1, q])
 
     def onward(b, q):
         here = out.at[pl.ds((ch * NWD + col_block(b)) * tokens + q * CHUNK, CHUNK)]
-        return remote(here, here, dev_y, fssem.at[b, q], frsem.at[b, q])
+        return remote(here, here, dev_y, fssem.at[0], frsem.at[b, q])
 
     def load_down(b, p):
         side = lax.rem(ch + p // DOWN, NCH)
@@ -679,20 +677,18 @@
 
     pass_results(2, 2 * DOWN, steps)
     pass_results(3, 0, steps)
+    unit_rows = 7 * LANES
     for g in range(blocks):
-        drain(g, first(g))
+        sent(ssem.at[g], unit_rows, 3 * width)
 
     @pl.loop(0, groups)
     def _(b):
-        drain(blocks + b, second(b))
-
-    for d in range(DOWN):
-        for kind in (OWN_X, OWN_Y, OWN_P, X_P, Y_P, Y_X, D_P):
-            down_piece(kind, d).wait_send()
+        sent(ssem.at[blocks + b], unit_rows, 2 * width)
+
+    sent(dssem.at[0], NCH, tokens, DOWN * 7 * deep * width // (NCH * tokens))
+    sent(xssem.at[0], tokens, 3 * width)
     by_core(lambda which: gate_over(which).wait_send())
-    for q in range(NX):
-        for p in (1, 2, 3):
-            x_copy(p, q).wait_send()
+    sent(ossem.at[0], tokens, 3 * width)
 
     @pl.when(core == 0)
     def _():
@@ -703,10 +699,11 @@
     @pl.loop(0, steps)
     def _(q):
         keep(q).wait()
-        across(q).wait()
+        across(q).wait_recv()
         for b in range(1, NWD):
-            direct(b, q).wait_send()
-            onward(b, q).wait()
+            onward(b, q).wait_recv()
+
+    sent(fssem.at[0], tokens, NWD * width)
 
 
 def put_out(src, dst, buf, isem, osem):
@@ -743,7 +740,6 @@
 
         dma = pltpu.SemaphoreType.DMA
         steps = rows // CHUNK
-        kinds = (8, blocks + groups, 3)
         outs = pl.pallas_call(
             layer,
             out_shape=[jax.ShapeDtypeStruct((tokens, width), BF16), like(w_y, False), like(w_x, False), like(w_o, True), like(w_g, False), like(w_u, False), like(w_d, True),
@@ -757,8 +753,8 @@
                             pltpu.VMEM((CHUNK + EDGE, LANES), F32), pltpu.VMEM((CHUNK, LANES), F32), pltpu.VMEM((CHUNK, LANES), F32),
                             pltpu.VMEM((EDGE, LANES), F32), pltpu.VMEM((SUB, LANES), F32),
                             pltpu.VMEM((total, EDGE + SUB, LANES), F32), pltpu.VMEM((total, EDGE + SUB, LANES), F32),
-                            dma(kinds), dma(kinds), dma((8, DOWN)), dma((8, DOWN)), dma((3, 2, NCH)), dma((2 * DOWN, 2)), dma((len(vectors),)), dma((3, NX)), dma((3, NX)), dma((7,)), dma((7,)), dma((15,)),
-                            dma((total,)), dma((total,)), dma((NWD,)), dma((3, steps)), dma((3, steps)), dma((4, steps)), dma((4, steps)), dma((steps,))],
+                            dma((blocks + groups,)), dma((8, blocks, 3)), dma((8, groups, 2)), dma((1,)), dma((8, DOWN)), dma((3, 2, NCH)), dma((2 * DOWN, 2)), dma((len(vectors),)), dma((1,)), dma((3, NX)), dma((6,)), dma((6,)), dma((15,)),
+                            dma((total,)), dma((total,)), dma((NWD,)), dma((1,)), dma((3, steps)), dma((1,)), dma((4, steps)), dma((steps,))],
             compiler_params=pltpu.CompilerParams(collective_id=0, has_side_effects=True, vmem_limit_bytes=VMEM_LIMIT),
             name="layer",
         )(resid_in, seg_pos, w_y, w_x, w_o, w_g, w_u, w_d, rgate_w.reshape(-1, LANES), igate_w.reshape(-1, LANES), *vectors)

time: 655 us -> 650 us (level)
  no operation moved by 1% of the time
where the time goes in v4:
time: 650 us
  Pallas kernels  650 us (100%)
    pallas_call x1, Pallas kernels, local_layer(): pl.pallas_call(layer, out_shape=[jax.ShapeDtypeStruct((tokens, width), BF...  638 us

profile of v4, /device:TPU:0, one launch (start us, length us, event | category | flops | bytes accessed | tf_op | source)
XLA Modules:
  0.0 649.9 jit_solution(7120767284997139479)
XLA Ops:
  0.0 638.1 %layer.1 = (bf16[16384,512]{1,0:T(8,128)(2,1)}, bf16[2,2048,1280]{2,1,0:T(8,128)(2,1)}, bf16[2,2048,1280]{2,1,0:T(8,128)(2,1)}, bf16[2,1280,2048]{2,1,0:T(8,128)...) custom-call(bf16[16384,512]{1,0:T(8,128)(2,1)} %resid.1, ...), custom_call_target="tpu_custom_call" | custom-call | tf_op jit(solution)/shard_map/layer/pallas_call | solution.py:743
  638.1 11.8 %put_out.1 = bf16[16384,512]{1,0:T(8,128)(2,1)} custom-call(bf16[16384,512]{1,0:T(8,128)(2,1)} %get-tuple-element.6.src), custom_call_target="tpu_custom_call" | custom-call | tf_op jit(solution)/shard_map/put_out/pallas_call | solution.py:761
